TPU v7x, 32 devices: a whole 2x2x4 slice. The times are simulated.
32 devices in a mesh: event: 2 (over x), draw: 8 (over z, y), bin: 2 (over core).
Axes of the slice: x: 2, y: 2, z: 4, core: 2. Of those that a mesh axis runs over, the one named last changes fastest.
Arguments:
- fine_cross: float32 [6, 2, 8192], P('event', None, 'draw'), parts along dimension 0, may hold values from -0.15 to 0.15
- fine_power: float32 [6, 8192], P('event', 'draw'), parts along dimension 0, may hold values from 0.000125 to 0.005
- bin_widths: int32 [256], P('event'), parts along dimension 0, may hold values from 1 to 128, 8192 in all
- log_amps: float32 [6, 8192], P('event', 'draw'), parts along dimension 0, may hold values from -0.5 to 0.5
- delays: float32 [6, 8192], P('event', 'draw'), parts along dimension 0, may hold values from -1.5 to 1.5
- phases: float32 [16384], P(('event', 'draw')), parts along dimension 0, may hold values from -3.140625 to 3.140625
- chirps: float32 [16384], P(('event', 'draw')), parts along dimension 0, may hold values from -8 to 8
- proposal_log: float32 [16384], P(('event', 'draw')), parts along dimension 0, may hold values from -100 to 130
Outputs:
- log_weights: float32 [16384], P(('event', 'draw')), parts along dimension 0
- log_evidence: float32 [2], P('event'), parts along dimension 0
There are 2 independent parts, one for each index of `event`. A program takes and returns all parts, laid end to end along the dimension named above; each array names one. Nothing has to cross between parts.
Inputs may be any that keep to these rules, and one draw needn't show every extreme that they name: `bin_widths`: the widths of an event sum to 8192; each is 1 to 128 and one is exactly 128.
All inputs are finite; a program needn't handle non-finite values.
Results may differ from a plain program's by a relative error of at most 0.00016.
Values sent between devices are 32-bit elements; how exact they have to be, the bound alone decides.
A program may use at most 64 MiB of HBM per device.

v0:
```python
import math

import jax
import jax.numpy as jnp
from jax import lax
from jax.sharding import PartitionSpec as P

FINE = 8192
TSHIFT = 2048


TWO_PI = 2.0 * math.pi
TIME_STEP = 0.125
PRECISE = lax.Precision.HIGHEST


def summary_terms(cross_rows, power_rows, first_fine, lower_edge, bin_widths):
    fine_index = first_fine + jnp.arange(power_rows.shape[1], dtype=jnp.int32)
    upper_edge = lower_edge + bin_widths
    inside = (
        (fine_index[:, None] >= lower_edge[None, :]) & (fine_index[:, None] < upper_edge[None, :])
    ).astype(jnp.float32)
    offset = fine_index.astype(jnp.float32)[:, None] + 0.5 - lower_edge.astype(jnp.float32)[None, :]
    weight = inside * offset / bin_widths.astype(jnp.float32)[None, :]
    lower_weight = inside - weight
    detectors = power_rows.shape[0]
    flattened = cross_rows.reshape(detectors * 2, -1)
    start_sums = jnp.dot(flattened, lower_weight, precision=PRECISE).reshape(detectors, 2, -1)
    end_sums = jnp.dot(flattened, weight, precision=PRECISE).reshape(detectors, 2, -1)
    power_low = jnp.dot(power_rows, lower_weight * lower_weight, precision=PRECISE)
    power_mixed = jnp.dot(power_rows, lower_weight * weight, precision=PRECISE)
    power_high = jnp.dot(power_rows, weight * weight, precision=PRECISE)
    return (start_sums, end_sums, power_low, power_mixed, power_high)


def edge_phase(freq_values, delays, phases, chirps):
    return (
        (TWO_PI * freq_values)[None, :, None] * delays[:, None, :]
        + phases[None, None, :]
        + chirps[None, None, :] * (freq_values * freq_values)[None, :, None]
    )


def sample_terms(
    freq_low, freq_high, log_amps, delays, phases, chirps, power_low, power_mixed, power_high
):
    amplitude = jnp.exp(log_amps)[:, None, :]
    phase_low = edge_phase(freq_low, delays, phases, chirps)
    phase_high = edge_phase(freq_high, delays, phases, chirps)
    pair_low = jnp.stack([amplitude * jnp.cos(phase_low), amplitude * jnp.sin(phase_low)], axis=2)
    pair_high = jnp.stack(
        [amplitude * jnp.cos(phase_high), amplitude * jnp.sin(phase_high)], axis=2
    )
    features = jnp.stack([pair_low, pair_high], axis=2).reshape(-1, log_amps.shape[1])
    cos_diff = jnp.cos(phase_low - phase_high)
    inner_sum = jnp.sum(power_low + power_high, axis=1)[:, None] + 2.0 * jnp.einsum(
        "db,dbn->dn", power_mixed, cos_diff, precision=PRECISE
    )
    self_power = jnp.sum(jnp.exp(2.0 * log_amps) * inner_sum, axis=0)
    return (features, self_power)


def build_table(row_count, total_shifts, start_sums, end_sums, freq_low, freq_high):
    shifts = (jnp.arange(row_count, dtype=jnp.int32) - total_shifts // 2).astype(
        jnp.float32
    ) * TIME_STEP
    edge_freq = jnp.stack([freq_low, freq_high], axis=-1)
    angles = (TWO_PI * edge_freq)[None] * shifts[:, None, None]
    cosine = jnp.cos(angles)[:, None]
    sine_value = jnp.sin(angles)[:, None]
    real_part = jnp.stack([start_sums[:, 0], end_sums[:, 0]], axis=-1)[None]
    imag_part = jnp.stack([start_sums[:, 1], end_sums[:, 1]], axis=-1)[None]
    table_real = real_part * cosine + imag_part * sine_value
    table_imag = imag_part * cosine - real_part * sine_value
    return jnp.stack([table_real, table_imag], axis=-1).reshape(row_count, -1)


def column_lse(scores):
    largest = jnp.max(scores, axis=0)
    return largest + jnp.log(jnp.sum(jnp.exp(scores - largest[None, :]), axis=0)) - math.log(TSHIFT)


def body(fine_cross, fine_power, bin_widths, log_amps, delays, phases, chirps, proposal_log):
    fine_count = fine_power.shape[1]
    first_fine = lax.axis_index("draw") * fine_count
    upper_edge = jnp.cumsum(bin_widths)
    lower_edge = upper_edge - bin_widths
    sample_count = log_amps.shape[1] // lax.axis_size("bin")
    sample_start = lax.axis_index("bin") * sample_count
    log_amps = lax.dynamic_slice_in_dim(log_amps, sample_start, sample_count, 1)
    delays = lax.dynamic_slice_in_dim(delays, sample_start, sample_count, 1)
    phases = lax.dynamic_slice_in_dim(phases, sample_start, sample_count, 0)
    chirps = lax.dynamic_slice_in_dim(chirps, sample_start, sample_count, 0)
    proposal_log = lax.dynamic_slice_in_dim(proposal_log, sample_start, sample_count, 0)
    upper_edge = lower_edge + bin_widths
    local_sums = summary_terms(fine_cross, fine_power, first_fine, lower_edge, bin_widths)
    start_sums, end_sums, power_low, power_mixed, power_high = lax.psum(
        (local_sums[0], local_sums[1], local_sums[2], local_sums[3], local_sums[4]), "draw"
    )
    freq_low = lower_edge.astype(jnp.float32) / FINE
    freq_high = upper_edge.astype(jnp.float32) / FINE
    features, self_power = sample_terms(
        freq_low, freq_high, log_amps, delays, phases, chirps, power_low, power_mixed, power_high
    )
    matrix = build_table(TSHIFT, TSHIFT, start_sums, end_sums, freq_low, freq_high)
    cross_terms = jnp.dot(matrix, features, precision=PRECISE)
    partial_value = cross_terms - 0.5 * self_power[None, :]
    scores = partial_value + proposal_log[None, :]
    marginal = lax.all_gather(column_lse(scores), "bin", axis=0, tiled=True)
    largest = lax.pmax(jnp.max(marginal), "draw")
    summed = lax.psum(jnp.sum(jnp.exp(marginal - largest)), "draw")
    total_log = largest + jnp.log(summed)
    total_draws = marginal.shape[0] * lax.axis_size("draw")
    return (marginal - total_log, (total_log - math.log(total_draws)).reshape(1))


def solution(mesh):
    placed = (
        P("event", None, "draw"),
        P("event", "draw"),
        P("event"),
        P("event", "draw"),
        P("event", "draw"),
        P(("event", "draw")),
        P(("event", "draw")),
        P(("event", "draw")),
    )
    return jax.shard_map(
        body,
        mesh=mesh,
        in_specs=placed,
        out_specs=(P(("event", "draw")), P("event")),
        check_vma=False,
    )
```

profile of v0, /device:TPU:0, one launch (start us, length us, event | category | flops | bytes accessed | tf_op | source)
XLA Modules:
  0.0 137.9 jit_solution(12257684062178921466)
XLA Ops:
  0.6 0.0 copy-start
  0.6 0.0 copy-start.2
  0.7 0.8 copy.22
  1.4 0.2 reduce-window.4
  1.6 0.1 reduce.2
  1.7 0.7 convert_multiply_fusion.1
  2.4 0.7 convert_element_type.48
  3.1 1.3 fusion.21
  4.4 0.0 copy-start.7
  4.4 1.4 %fusion.9 = f32[3,128]{1,0:T(4,128)S(1)} fusion(f32[128,3]{0,1:T(4,128)S(1)} %fusion.21, f32[3,1024]{1,0:T(4,128)} %param.9, f32[128]{0:T(128)S(1)} %convert_element_type.48, f32[128]{0:T(128)S(1)} %convert_element_type.47, f32[1024]{0:T(1024)S(1)} %convert_add_fusion, s32[128]{0:T(128)S(1)} %reduce.2, s32[128]{0:T(128)S(1)} %get-tuple-element.31, ...), kind=kOutput, calls=%fused_computation.21 | convolution fusion | flops 5636480 | bytes 25600 | tf_op jit(solution)/shard_map/dot_general | solution.py:32
  5.8 0.0 copy-done.2
  5.9 0.6 convolution_bitcast_fusion.1
  6.5 0.6 convolution_bitcast_fusion
  7.1 0.0 copy-done.7
  7.1 0.6 convolution_bitcast_fusion.2
  7.8 38.9 %all-reduce = (f32[3,2,128]{2,1,0:T(2,128)S(1)}, f32[3,2,128]{2,1,0:T(2,128)S(1)}, f32[3,128]{1,0:T(4,128)S(1)}, f32[3,128]{1,0:T(4,128)S(1)}) all-reduce(f32[3,2,128]{2,1,0:T(2,128)S(1)} %reshape.217, f32[3,2,128]{2,1,0:T(2,128)S(1)} %reshape.216, ...), channel_id=1, replica_groups=mesh['event'=2,'draw'=8,'bin'=2] {'draw'}, use_global_device_ids=true, to_apply=%region_2.3 | all-reduce | flops 2304 | bytes 18432 | tf_op jit(solution)/shard_map/psum | solution.py:97
  46.7 0.1 copy.23
  46.8 7.3 %multiply_cosine_fusion = (f32[2048,128,2]{1,0,2:T(8,128)S(1)}, f32[2048,128,2]{1,0,2:T(8,128)S(1)}) fusion(f32[2048]{0:T(1024)S(1)} %convert_multiply_fusion, f32[128,2]{0,1:T(2,128)S(1)} %maximum_multiply_fusion), kind=kLoop, calls=%fused_computation.14 | loop fusion | flops 524288 | bytes 4203520 | tf_op jit(solution)/shard_map/cos | solution.py:69
  54.1 0.0 copy-start.4
  54.1 0.0 copy-start.5
  54.1 0.0 copy-start.3
  54.2 6.1 %multiply_add_fusion = (f32[2048,3,128,2,1]{2,0,4,3,1:T(8,128)}, f32[2048,3,128,2,1]{2,0,4,3,1:T(8,128)}) fusion(f32[2048,128,2]{1,0,2:T(8,128)S(1)} %get-tuple-element.19, f32[3,128,2]{1,2,0:T(2,128)S(1)} %pad_maximum_fusion.1, f32[2048,128,2]{1,0,2:T(8,128)S(1)} %get-tuple-element.18, f32[3,128,2]{1,2,0:T(2,128)S(1)} %pad_maximum_fusion), kind=kLoop, calls=%fused_computation.5 | loop fusion | flops 9437184 | bytes 16783360 | tf_op jit(solution)/shard_map/add | solution.py:73
  60.2 0.0 copy-done.4
  60.2 0.1 dynamic_slice.18
  60.3 0.1 broadcast_multiply_fusion.1
  60.4 0.0 copy-done
  60.5 0.0 copy-done.5
  60.5 0.1 dynamic_slice.17
  60.5 3.4 %fusion.10 = f32[3,1,512]{2,1,0:T(1,128)S(1)} fusion(f32[128,512]{1,0:T(8,128)S(1)} %get-tuple-element.25, f32[128]{0:T(128)S(1)} %get-tuple-element.28, f32[128,512]{1,0:T(8,128)S(1)} %get-tuple-element.24, f32[512]{0:T(512)S(1)} %dynamic_slice.17, f32[3,512]{1,0:T(4,128)S(1)} %constant_dynamic-slice_fusion, f32[128]{0:T(128)S(1)} %get-tuple-element.30, ...), kind=kOutput, calls=%fused_computation.22 | convolution fusion | flops 3735552 | bytes 541184 | tf_op jit(solution)/shard_map/db,dbn->dn/dot_general | solution.py:56
  64.0 0.1 reduce_sum.36
  64.1 0.0 copy-done.3
  64.1 0.1 fusion.31
  64.2 0.0 copy-start.6
  64.2 0.0 copy-start.1
  64.2 5.7 %cosine_multiply_fusion.1 = (f32[3,128,1,512]{3,1,2,0:T(8,128)S(1)}, f32[3,128,1,512]{3,1,2,0:T(8,128)S(1)}, f32[3,128,1,512]{3,1,2,0:T(8,128)S(1)}, f32[3,128,1,512]{3,1,2,0:T(8,128)S(1)}) fusion(f32[128,512]{1,0:T(8,128)S(1)} %get-tuple-element.24, f32[512]{0:T(512)S(1)} %dynamic_slice.17, f32[3,512]{1,0:T(4,128)S(1)} %constant_dynamic-slice_fusion, ...), kind=kLoop, calls=%fused_computation.35 | loop fusion | flops 1966080 | bytes 3685376 | tf_op jit(solution)/shard_map/mul | solution.py:50
  69.9 0.3 maximum_bitcast_fusion
  70.2 0.0 copy-done.6
  70.2 0.1 dynamic_slice.19
  70.3 0.0 copy-done.1
  70.3 22.4 %fusion.5 = (f32[512]{0:T(512)S(1)}, f32[2048,512,1,1,1]{1,0,4,3,2:T(8,128)S(1)}) fusion(f32[512]{0:T(512)S(1)} %dynamic_slice.19, f32[512]{0:T(512)S(1)} %broadcast_multiply_fusion.2, f32[3,128,1,2,512]{4,1,3,2,0:T(8,128)S(1)} %get-tuple-element.37, f32[3,128,1,2,512]{4,1,3,2,0:T(8,128)S(1)} %get-tuple-element.36, ...), kind=kOutput, calls=%fused_computation.9 | convolution fusion | flops 19334430720 | bytes 19929088 | tf_op jit(solution)/shard_map/dot_general | solution.py:106
  92.7 0.9 exponential_reduce_fusion
  93.6 1.8 %all-gather = f32[2,1,512]{2,1,0:T(1,128)S(1)} all-gather(f32[1,1,512]{2,1,0:T(1,128)S(1)} %bitcast.52), channel_id=1, replica_groups=mesh['event'=2,'draw'=8,'bin'=2] {'bin'}, dimensions={0}, use_global_device_ids=true | all-gather | bytes 6144 | tf_op jit(solution)/shard_map/all_gather | solution.py:109
  95.4 0.6 reduce_max.19
  96.0 17.7 %pmax.7 = f32[]{:T(128)} all-reduce(f32[]{:T(128)} %reduce_max.19), channel_id=1, replica_groups=mesh['event'=2,'draw'=8,'bin'=2] {'draw'}, use_global_device_ids=true, to_apply=%region_11.12 | all-reduce | flops 1 | bytes 8 | tf_op jit(solution)/shard_map/pmax | solution.py:110
  113.8 1.3 exponential_reduce_fusion.1
  115.1 19.7 %psum.47 = f32[]{:T(128)} all-reduce(f32[]{:T(128)} %exponential_reduce_fusion.1), channel_id=1, replica_groups=mesh['event'=2,'draw'=8,'bin'=2] {'draw'}, use_global_device_ids=true, to_apply=%region_13.14 | all-reduce | flops 1 | bytes 8 | tf_op jit(solution)/shard_map/psum | solution.py:111
  136.1 0.6 broadcast_subtract_fusion
  (16 shorter events, 0.2 us)
Async XLA Ops:
  0.6 59.8 %copy-start = (f32[3,1024]{1,0:T(4,128)S(1)}, f32[3,1024]{1,0:T(4,128)}, u32[]{:S(2)}) copy-start(f32[3,1024]{1,0:T(4,128)} %param.12) | copy-start | bytes 36868
  0.6 5.2 %copy-start.2 = (f32[3,2,1024]{2,1,0:T(2,128)S(1)}, f32[3,2,1024]{2,1,0:T(2,128)}, u32[]{:S(2)}) copy-start(f32[3,2,1024]{2,1,0:T(2,128)} %param.8) | copy-start | bytes 73732
  4.4 2.7 %copy-start.7 = (f32[3,1024]{1,0:T(4,128)S(1)}, f32[3,1024]{1,0:T(4,128)}, u32[]{:S(2)}) copy-start(f32[3,1024]{1,0:T(4,128)} %param.9) | copy-start | bytes 36868
  54.1 6.1 %copy-start.4 = (f32[1024]{0:T(1024)S(1)}, f32[1024]{0:T(1024)}, u32[]{:S(2)}) copy-start(f32[1024]{0:T(1024)} %param.14) | copy-start | bytes 12292
  54.1 6.3 %copy-start.5 = (f32[1024]{0:T(1024)S(1)}, f32[1024]{0:T(1024)}, u32[]{:S(2)}) copy-start(f32[1024]{0:T(1024)} %param.13) | copy-start | bytes 12292
  54.1 9.9 %copy-start.3 = (f32[3,1024]{1,0:T(4,128)S(1)}, f32[3,1024]{1,0:T(4,128)}, u32[]{:S(2)}) copy-start(f32[3,1024]{1,0:T(4,128)} %param.11) | copy-start | bytes 36868
  64.2 6.0 %copy-start.6 = (f32[1024]{0:T(1024)S(1)}, f32[1024]{0:T(1024)}, u32[]{:S(2)}) copy-start(f32[1024]{0:T(1024)} %param.15) | copy-start | bytes 12292
  64.2 6.1 %copy-start.1 = (f32[2048,3,128,2,1]{2,0,4,3,1:T(8,128)S(1)}, f32[2048,3,128,2,1]{2,0,4,3,1:T(8,128)}, u32[]{:S(2)}) copy-start(f32[2048,3,128,2,1]{2,0,4,3,1:T(8,128)} %get-tuple-element.8) | copy-start | bytes 18874372
where the time goes:
time: 138 us
  blocking collectives  78.2 us (57%)
  matrix products  30.4 us (22%)
  other arithmetic  24.8 us (18%)
  between operations  3.32 us (2%)
    psum x1, blocking collectives, body(): lax.psum((local_sums[0], local_sums[1], local_sums[2], local_sums[3], loc...  38.9 us
    dot_general x1, matrix products, body(): cross_terms = jnp.dot(matrix, features, precision=PRECISE)  22.4 us
    psum x1, blocking collectives, body(): summed = lax.psum(jnp.sum(jnp.exp(marginal - largest)), 'draw')  19.7 us
    pmax x1, blocking collectives, body(): largest = lax.pmax(jnp.max(marginal), 'draw')  17.7 us
    cos x1, other arithmetic, build_table(): cosine = jnp.cos(angles)[:, None]  7.3 us
    add x1, other arithmetic, build_table(): table_real = real_part * cosine + imag_part * sine_value  6.08 us
    mul x1, other arithmetic, sample_terms(): amplitude * jnp.cos(phase_low)  5.71 us
    dot_general x1, matrix products, sample_terms(): jnp.einsum('db,dbn->dn', power_mixed, cos_diff, precision=PRECISE)  3.42 us

commit v1 on v0

v1 whole, which is shorter than its diff:
```python
import functools
import math

import jax
import jax.numpy as jnp
import numpy as np
from jax import lax
from jax.experimental import pallas as pl
from jax.experimental.pallas import tpu as pltpu
from jax.sharding import PartitionSpec as P

TSHIFT = 2048
STEPS_PER_UNIT = 8
LOG2E = math.log2(math.e)
LN2 = math.log(2.0)
LANES = 128
ROWS = 16
CHUNK = 128
F32 = jnp.float32
BF16 = jnp.bfloat16


def even_fit(func, terms):
    nodes = 0.125 * (1.0 + np.cos(np.pi * (np.arange(64) + 0.5) / 64))
    values = func(np.sqrt(nodes))
    fit = np.polynomial.chebyshev.Chebyshev.fit(nodes, values, terms - 1, domain=[0.0, 0.25])
    return [float(c) for c in fit.convert(kind=np.polynomial.Polynomial).coef]


SIN_COEF = even_fit(lambda u: np.sin(np.pi * u) / u, 6)
COS_COEF = even_fit(lambda u: np.cos(np.pi * u), 6)


def horner(z, coefs):
    total = jnp.full_like(z, coefs[-1])
    for c in coefs[-2::-1]:
        total = total * z + c
    return total


def cos_sin_turns(t):
    u = t - jnp.round(t)
    z = u * u
    s = u * horner(z, SIN_COEF)
    c = horner(z, COS_COEF)
    return 1.0 - 2.0 * (s * s), 2.0 * (s * c)


def halves(x):
    hi = x.astype(BF16)
    lo = (x - hi.astype(F32)).astype(BF16)
    return hi, lo


def each(count, step):
    if count <= 16:
        for i in range(count):
            step(i)
    else:
        lax.fori_loop(0, count, lambda i, c: (step(i), c)[1], 0)


def kernel(n_draw, n_bin, cross_ref, power_ref, width_ref, amp_ref, delay_ref, phase_ref, chirp_ref, prop_ref,
           out_ref, evid_ref, sums, packets, ctab, stab, acos, asin, cdiff, zr, zi, xcol, coef, base_ref,
           send1, recv1, send2, recv2):
    n_all = n_draw * n_bin
    my_draw, my_bin = lax.axis_index("draw"), lax.axis_index("bin")
    me = my_draw * n_bin + my_bin
    dets = power_ref.shape[0]
    fine = power_ref.shape[1]
    bins = width_ref.shape[1]
    half = phase_ref.shape[1] // n_bin
    grid_fine = fine * n_draw
    turns = 1.0 / (grid_fine * STEPS_PER_UNIT * 2)

    barrier = pltpu.get_barrier_semaphore()

    def greet(r):
        other = lax.rem(me + 1 + r, n_all)
        pl.semaphore_signal(barrier, inc=1, device_id={"draw": other // n_bin, "bin": lax.rem(other, n_bin)},
                            device_id_type=pl.DeviceIdType.MESH)

    each(n_all - 1, greet)

    width_row = width_ref[...].astype(F32)
    row_id = lax.broadcasted_iota(jnp.int32, (bins, bins), 0)
    lane_id = lax.broadcasted_iota(jnp.int32, (bins, bins), 1)
    wide = jnp.broadcast_to(width_row, (bins, bins))
    lower = jnp.sum(jnp.where(lane_id < row_id, wide, 0.0), axis=1, keepdims=True)
    width = jnp.sum(jnp.where(lane_id == row_id, wide, 0.0), axis=1, keepdims=True)
    upper_row = jnp.sum(jnp.where(row_id <= lane_id, jnp.broadcast_to(width, (bins, bins)), 0.0), axis=0, keepdims=True)
    xcol[...] = jnp.broadcast_to((lower + width) * (1.0 / grid_fine), (bins, LANES))

    first = (my_draw * fine).astype(F32)
    pos = lax.broadcasted_iota(jnp.int32, (bins, fine), 1).astype(F32) + (first + 0.5)
    off = pos - lower
    inside = (off > 0.0) & (off < width)
    onehot = jnp.where(inside, 1.0, 0.0).astype(BF16)
    w = jnp.sum(jnp.where(inside, off * (1.0 / width), 0.0), axis=0, keepdims=True)
    v = 1.0 - w
    crosses = [cross_ref[d] for d in range(dets)]
    power = power_ref[...]
    data = jnp.concatenate([c * v for c in crosses] + [c * w for c in crosses] + [power * (w * v)]
                           + [jnp.zeros((ROWS - 5 * dets, fine), F32)], axis=0)
    d0 = data.astype(BF16)
    rest = data - d0.astype(F32)
    d1 = rest.astype(BF16)
    d2 = (rest - d1.astype(F32)).astype(BF16)
    parts = lax.dot_general(jnp.concatenate([d0, d1, d2], axis=0), onehot, (((1,), (1,)), ((), ())),
                            preferred_element_type=F32)
    local = parts[:ROWS] + (parts[ROWS:2 * ROWS] + parts[2 * ROWS:])
    flat = jnp.sum(power * (v * v + w * w), axis=1, keepdims=True)
    lane_row = lax.broadcasted_iota(jnp.int32, (1, bins), 1)
    ends = jnp.zeros((1, bins), F32)
    for d in range(dets):
        ends = jnp.where(lane_row == d, flat[d:d + 1], ends)
    sub16 = lax.broadcasted_iota(jnp.int32, (ROWS, bins), 0)
    sums[my_draw] = jnp.where(sub16 == ROWS - 1, ends, local)

    pl.semaphore_wait(barrier, n_all - 1)

    def sum_copy(slot, dev):
        return pltpu.make_async_remote_copy(
            src_ref=sums.at[slot], dst_ref=sums.at[slot], send_sem=send1.at[dev], recv_sem=recv1.at[slot],
            device_id={"draw": dev, "bin": my_bin}, device_id_type=pl.DeviceIdType.MESH)

    each(n_draw - 1, lambda r: sum_copy(my_draw, lax.rem(my_draw + 1 + r, n_draw)).start())

    def table_rows(i, carry):
        at = pl.multiple_of(i * 16, 16)
        odd = (2 * (lax.broadcasted_iota(jnp.int32, (16, bins), 0) + at) + 1).astype(F32)
        c, s = cos_sin_turns(odd * upper_row * turns)
        ch, cl = halves(c)
        sh, sl = halves(s)
        ctab[pl.ds(at, 16), :] = jnp.concatenate([ch, ch, cl, cl], axis=1)
        stab[pl.ds(at, 16), :] = jnp.concatenate([sh, sh, sl, sl], axis=1)
        return carry

    lax.fori_loop(0, TSHIFT // 32, table_rows, 0)

    mine = pl.ds(pl.multiple_of(my_bin * half, half), half)
    amp = [jnp.exp(amp_ref[d:d + 1, mine]) for d in range(dets)]
    delay = [delay_ref[d:d + 1, mine] for d in range(dets)]
    phase = phase_ref[:, mine] * (1.0 / (2.0 * math.pi))
    chirp = chirp_ref[:, mine] * (1.0 / (2.0 * math.pi))
    cos0, sin0 = cos_sin_turns(phase)
    twice = [2.0 * a * a for a in amp]
    sub8 = lax.broadcasted_iota(jnp.int32, (8, half), 0)
    seeds = tuple(jnp.broadcast_to(x, (8, half)) for _ in range(dets) for x in (cos0, sin0))

    def feature_rows(i, carry):
        at = pl.multiple_of(i * 8, 8)
        x = xcol[pl.ds(at, 8), 0:1]
        shared = phase + chirp * (x * x)
        new = []
        for d in range(dets):
            c, s = cos_sin_turns(x * delay[d] + shared)
            cr, sr = pltpu.roll(c, 1, 0), pltpu.roll(s, 1, 0)
            cp = jnp.where(sub8 == 0, carry[2 * d], cr)
            sp = jnp.where(sub8 == 0, carry[2 * d + 1], sr)
            new += [cr, sr]
            cdiff[d, pl.ds(at, 8), :] = (c * cp + s * sp) * twice[d]
            acos[d, pl.ds(at, 8), :] = c * amp[d]
            asin[d, pl.ds(at, 8), :] = s * amp[d]
        return tuple(new)

    lax.fori_loop(0, bins // 8, feature_rows, seeds)

    each(n_draw - 1, lambda r: sum_copy(lax.rem(my_draw + 1 + r, n_draw), my_draw).wait_recv())
    total = sums[0]
    for i in range(1, n_draw):
        total = total + sums[i]

    start, end = total[:2 * dets], total[2 * dets:4 * dets]
    both = end + jnp.where(lane_row < bins - 1, pltpu.roll(total, bins - 1, 1)[:2 * dets], 0.0)
    rc, rs = cos_sin_turns(upper_row * turns)
    rc, rs = rc * LOG2E, rs * LOG2E
    rows = []
    for d in range(dets):
        re, im = both[2 * d:2 * d + 1], both[2 * d + 1:2 * d + 2]
        rows += [re * rc - im * rs, im * rc + re * rs]
    rows += [total[4 * dets + d:4 * dets + d + 1] for d in range(dets)]
    rows.append(jnp.zeros((LANES - len(rows), bins), F32))
    coef[...] = jnp.concatenate(rows, axis=0).T

    zero = jnp.zeros((8, half), F32)

    def mix_rows(i, power_sum):
        out_r, out_i = [], []
        for k in range(2):
            at = pl.multiple_of(i * 16 + 8 * k, 8)
            re = im = None
            for d in range(dets):
                ac, as_ = acos[d, pl.ds(at, 8), :], asin[d, pl.ds(at, 8), :]
                cr, ci = coef[pl.ds(at, 8), 2 * d:2 * d + 1], coef[pl.ds(at, 8), 2 * d + 1:2 * d + 2]
                r, m = cr * ac + ci * as_, ci * ac - cr * as_
                re, im = (r, m) if re is None else (re + r, im + m)
                pm = coef[pl.ds(at, 8), 2 * dets + d:2 * dets + d + 1]
                power_sum = power_sum + pm * cdiff[d, pl.ds(at, 8), :]
            out_r.append(re)
            out_i.append(im)
        for ref, val in ((zr, out_r), (zi, out_i)):
            hi, lo = halves(jnp.concatenate(val, axis=0))
            for part, block in enumerate((hi, lo, hi, lo)):
                ref[pl.ds(pl.multiple_of(part * bins + i * 16, 16), 16), :] = block
        return power_sum

    self_power = jnp.sum(lax.fori_loop(0, bins // 16, mix_rows, zero), axis=0, keepdims=True)
    fixed = jnp.zeros((1, half), F32)
    for d in range(dets):
        self_power = self_power + (0.5 * twice[d]) * total[ROWS - 1:ROWS, d:d + 1]
        fixed = fixed + amp[d] * (start[2 * d:2 * d + 1, 0:1] * cos0 + start[2 * d + 1:2 * d + 2, 0:1] * sin0)
    base_ref[...] = fixed - 0.5 * self_power + prop_ref[:, mine] - math.log(TSHIFT)

    top = jnp.full((8, half), -jnp.inf, F32)
    acc = zero
    for i in range(TSHIFT // 2 // CHUNK):
        a = jnp.dot(ctab[i * CHUNK:(i + 1) * CHUNK, :], zr[...], preferred_element_type=F32)
        b = jnp.dot(stab[i * CHUNK:(i + 1) * CHUNK, :], zi[...], preferred_element_type=F32)
        a = a.reshape(CHUNK // 8, 8, half)
        b = b.reshape(CHUNK // 8, 8, half)
        p, q = a + b, a - b
        new = jnp.maximum(top, jnp.max(jnp.maximum(p, q), axis=0))
        acc = acc * jnp.exp2(top - new) + jnp.sum(jnp.exp2(p - new[None]) + jnp.exp2(q - new[None]), axis=0)
        top = new
    peak = jnp.max(top, axis=0, keepdims=True)
    mass = jnp.sum(acc * jnp.exp2(top - peak), axis=0, keepdims=True)
    marginal = peak * LN2 + jnp.log(mass) + base_ref[...]

    largest = jnp.max(marginal, axis=1, keepdims=True)
    scaled = jnp.sum(jnp.exp(marginal - largest), axis=1, keepdims=True)
    count = half // LANES
    used = [marginal[:, i * LANES:(i + 1) * LANES] for i in range(count)]
    used += [jnp.broadcast_to(largest, (1, LANES)), jnp.broadcast_to(scaled, (1, LANES))]
    pad = packets.shape[1] - len(used)
    packets[me] = jnp.concatenate(used + [jnp.zeros((pad, LANES), F32)], axis=0)

    def packet_copy(slot, dev):
        return pltpu.make_async_remote_copy(
            src_ref=packets.at[slot], dst_ref=packets.at[slot], send_sem=send2.at[dev], recv_sem=recv2.at[slot],
            device_id={"draw": dev // n_bin, "bin": lax.rem(dev, n_bin)}, device_id_type=pl.DeviceIdType.MESH)

    each(n_all - 1, lambda r: packet_copy(me, lax.rem(me + 1 + r, n_all)).start())
    each(n_all - 1, lambda r: packet_copy(lax.rem(me + 1 + r, n_all), me).wait_recv())

    tops = packets[:, count, :]
    masses = packets[:, count + 1, :]
    whole_top = jnp.max(tops, axis=0, keepdims=True)
    whole = jnp.sum(masses * jnp.exp(tops - whole_top), axis=0, keepdims=True)
    total_log = whole_top + jnp.log(whole)
    for q in range(n_bin):
        out_ref[q * count:(q + 1) * count, :] = packets[my_draw * n_bin + q, 0:count, :] - total_log
    evid_ref[...] = total_log[:, 0:1] - math.log(half * n_all)

    each(n_draw - 1, lambda r: sum_copy(my_draw, lax.rem(my_draw + 1 + r, n_draw)).wait_send())
    each(n_all - 1, lambda r: packet_copy(me, lax.rem(me + 1 + r, n_all)).wait_send())


def body(n_draw, n_bin, fine_cross, fine_power, bin_widths, log_amps, delays, phases, chirps, proposal_log):
    dets = fine_power.shape[0]
    bins = bin_widths.shape[0]
    draws = phases.shape[0]
    half = draws // n_bin
    n_all = n_draw * n_bin
    packet_rows = -(-(half // LANES + 2) // 8) * 8
    vmem = pl.BlockSpec(memory_space=pltpu.VMEM)
    weights, evidence = pl.pallas_call(
        functools.partial(kernel, n_draw, n_bin),
        out_shape=(jax.ShapeDtypeStruct((draws // LANES, LANES), F32), jax.ShapeDtypeStruct((1, 1), F32)),
        in_specs=[vmem] * 8,
        out_specs=(vmem, vmem),
        scratch_shapes=[
            pltpu.VMEM((n_draw, ROWS, bins), F32),
            pltpu.VMEM((n_all, packet_rows, LANES), F32),
            pltpu.VMEM((TSHIFT // 2, 4 * bins), BF16),
            pltpu.VMEM((TSHIFT // 2, 4 * bins), BF16),
            pltpu.VMEM((dets, bins, half), F32),
            pltpu.VMEM((dets, bins, half), F32),
            pltpu.VMEM((dets, bins, half), F32),
            pltpu.VMEM((4 * bins, half), BF16),
            pltpu.VMEM((4 * bins, half), BF16),
            pltpu.VMEM((bins, LANES), F32),
            pltpu.VMEM((bins, LANES), F32),
            pltpu.VMEM((1, half), F32),
            pltpu.SemaphoreType.DMA((n_draw,)),
            pltpu.SemaphoreType.DMA((n_draw,)),
            pltpu.SemaphoreType.DMA((n_all,)),
            pltpu.SemaphoreType.DMA((n_all,)),
        ],
        compiler_params=pltpu.CompilerParams(collective_id=0, has_side_effects=True),
        name="evidence",
    )(fine_cross, fine_power, bin_widths.reshape(1, bins), log_amps, delays, phases.reshape(1, draws),
      chirps.reshape(1, draws), proposal_log.reshape(1, draws))
    return weights.reshape(draws), evidence.reshape(1)


def solution(mesh):
    placed = (
        P("event", None, "draw"),
        P("event", "draw"),
        P("event"),
        P("event", "draw"),
        P("event", "draw"),
        P(("event", "draw")),
        P(("event", "draw")),
        P(("event", "draw")),
    )
    return jax.shard_map(
        functools.partial(body, mesh.shape["draw"], mesh.shape["bin"]),
        mesh=mesh,
        in_specs=placed,
        out_specs=(P(("event", "draw")), P("event")),
        check_vma=False,
    )
```

time: 138 us -> 23 us (0.17)
  blocking collectives: 78.2 us -> 0 us
  matrix products: 30.4 us -> 0 us
  other arithmetic: 24.8 us -> 0 us
  Pallas kernels: 0 us -> 19 us
    psum x2 -> x0, blocking collectives: 58.6 us -> none  [the longest x1 38.9 us: body(): lax.psum((local_sums[0], local_sums[1], local_sums[2], local_sums[3], loc...]
    dot_general x7 -> x0, matrix products: 30.4 us -> none  [the longest x1 22.4 us: body(): cross_terms = jnp.dot(matrix, features, precision=PRECISE)]
    pallas_call x0 -> x1, Pallas kernels: none -> 19 us  [body(): pl.pallas_call(functools.partial(kernel, n_draw, n_bin), out_shape=(jax.S...]
    pmax x1 -> x0, blocking collectives: 17.7 us -> none  [body(): largest = lax.pmax(jnp.max(marginal), 'draw')]
    cos x1 -> x0, other arithmetic: 7.3 us -> none  [build_table(): cosine = jnp.cos(angles)[:, None]]
    mul x7 -> x0, other arithmetic: 6.52 us -> none  [the longest x1 5.71 us: sample_terms(): amplitude * jnp.cos(phase_low)]
    add x3 -> x0, other arithmetic: 6.1 us -> none  [the longest x1 6.08 us: build_table(): table_real = real_part * cosine + imag_part * sine_value]
    reduce_sum x4 -> x0, other arithmetic: 2.35 us -> none  [the longest x1 1.26 us: body(): summed = lax.psum(jnp.sum(jnp.exp(marginal - largest)), 'draw')]
where the time goes in v1:
time: 23 us; the launch traced here: 22.7 us
  Pallas kernels  19 us (83%)
  between operations  2.41 us (10%)
  local copies, waits for them, and re-layouts  1.26 us (5%)
    pallas_call x1, Pallas kernels, body(): pl.pallas_call(functools.partial(kernel, n_draw, n_bin), out_shape=(jax.S...  19 us
    unnamed x3, local copies, waits for them, and re-layouts  1.26 us

profile of v1, /device:TPU:0, one launch (start us, length us, event | category | flops | bytes accessed | tf_op | source)
XLA Modules:
  0.0 22.7 jit_solution(937072843865948425)
XLA Ops:
  0.6 19.0 %evidence.1 = (f32[8,128]{1,0:T(8,128)}, f32[1,1]{1,0:T(1,128)}) custom-call(f32[3,2,1024]{2,1,0:T(2,128)} %cross_ref.1, f32[3,1024]{1,0:T(4,128)} %power_ref.1, s32[1,128]{1,0:T(1,128)} %bitcast.10, f32[3,1024]{1,0:T(4,128)} %amp_ref.1, f32[3,1024]{1,0:T(4,128)} %delay_ref.1, f32[1,1024]{1,0:T(1,128)} %bitcast.7, f32[1,1024]{1,0:T(1,128)} %bitcast.8, ...), custom_call_target="tpu_custom_call" | custom-call | tf_op jit(solution)/shard_map/evidence/pallas_call | solution.py:267
  19.7 0.0 copy-start
  19.7 0.7 %copy-done = f32[8,128]{1,0:T(8,128)S(1)} copy-done((f32[8,128]{1,0:T(8,128)S(1)}, f32[8,128]{1,0:T(8,128)}, u32[]{:S(2)}) %copy-start) | copy-done | bytes 4120
  20.4 0.6 %copy.12 = f32[1024]{0:T(1024)} copy(f32[1024]{0:T(1024)S(1)} %bitcast.6) | data formatting | bytes 8192
Async XLA Ops:
  19.7 0.7 %copy-start = (f32[8,128]{1,0:T(8,128)S(1)}, f32[8,128]{1,0:T(8,128)}, u32[]{:S(2)}) copy-start(f32[8,128]{1,0:T(8,128)} %get-tuple-element.4) | copy-start | bytes 12292

commit v2 on v1

--- a/solution.py
+++ b/solution.py
@@ -60,9 +60,15 @@
         lax.fori_loop(0, count, lambda i, c: (step(i), c)[1], 0)
 
 
-def kernel(n_draw, n_bin, cross_ref, power_ref, width_ref, amp_ref, delay_ref, phase_ref, chirp_ref, prop_ref,
-           out_ref, evid_ref, sums, packets, ctab, stab, acos, asin, cdiff, zr, zi, xcol, coef, base_ref,
-           send1, recv1, send2, recv2):
+def kernel(n_draw, n_bin, cross_in, power_in, width_in, amp_in, delay_in, phase_in, chirp_in, prop_in,
+           out_ref, evid_ref, cross_ref, power_ref, width_ref, amp_ref, delay_ref, phase_ref, chirp_ref, prop_ref,
+           sums, stats, margs, ctab, stab, acos, asin, cdiff, zr, zi, xcol, coef, base_ref,
+           load_sem, send1, recv1, send2, recv2, send3, recv3):
+    loads = [pltpu.make_async_copy(src, dst, load_sem.at[i]) for i, (src, dst) in enumerate((
+        (width_in, width_ref), (cross_in, cross_ref), (power_in, power_ref), (amp_in, amp_ref), (delay_in, delay_ref),
+        (phase_in, phase_ref), (chirp_in, chirp_ref), (prop_in, prop_ref)))]
+    for load in loads:
+        load.start()
     n_all = n_draw * n_bin
     my_draw, my_bin = lax.axis_index("draw"), lax.axis_index("bin")
     me = my_draw * n_bin + my_bin
@@ -82,6 +88,9 @@
 
     each(n_all - 1, greet)
 
+    for load in loads[:3]:
+        load.wait()
+
     width_row = width_ref[...].astype(F32)
     row_id = lax.broadcasted_iota(jnp.int32, (bins, bins), 0)
     lane_id = lax.broadcasted_iota(jnp.int32, (bins, bins), 1)
@@ -90,6 +99,16 @@
     width = jnp.sum(jnp.where(lane_id == row_id, wide, 0.0), axis=1, keepdims=True)
     upper_row = jnp.sum(jnp.where(row_id <= lane_id, jnp.broadcast_to(width, (bins, bins)), 0.0), axis=0, keepdims=True)
     xcol[...] = jnp.broadcast_to((lower + width) * (1.0 / grid_fine), (bins, LANES))
+
+    def table_rows(i, carry):
+        at = pl.multiple_of(i * 16, 16)
+        odd = (2 * (lax.broadcasted_iota(jnp.int32, (16, bins), 0) + at) + 1).astype(F32)
+        c, s = cos_sin_turns(odd * upper_row * turns)
+        ch, cl = halves(c)
+        sh, sl = halves(s)
+        ctab[pl.ds(at, 16), :] = jnp.concatenate([ch, ch, cl, cl], axis=1)
+        stab[pl.ds(at, 16), :] = jnp.concatenate([sh, sh, sl, sl], axis=1)
+        return carry
 
     first = (my_draw * fine).astype(F32)
     pos = lax.broadcasted_iota(jnp.int32, (bins, fine), 1).astype(F32) + (first + 0.5)
@@ -109,14 +128,19 @@
     parts = lax.dot_general(jnp.concatenate([d0, d1, d2], axis=0), onehot, (((1,), (1,)), ((), ())),
                             preferred_element_type=F32)
     local = parts[:ROWS] + (parts[ROWS:2 * ROWS] + parts[2 * ROWS:])
+    lane_row = lax.broadcasted_iota(jnp.int32, (1, bins), 1)
+    start, end = local[:2 * dets], local[2 * dets:4 * dets]
+    both = end + jnp.where(lane_row < bins - 1, pltpu.roll(local, bins - 1, 1)[:2 * dets], 0.0)
     flat = jnp.sum(power * (v * v + w * w), axis=1, keepdims=True)
-    lane_row = lax.broadcasted_iota(jnp.int32, (1, bins), 1)
     ends = jnp.zeros((1, bins), F32)
     for d in range(dets):
         ends = jnp.where(lane_row == d, flat[d:d + 1], ends)
-    sub16 = lax.broadcasted_iota(jnp.int32, (ROWS, bins), 0)
-    sums[my_draw] = jnp.where(sub16 == ROWS - 1, ends, local)
-
+    for r in range(2 * dets):
+        ends = jnp.where(lane_row == dets + r, start[r:r + 1, 0:1], ends)
+    packed = [both, local[4 * dets:5 * dets], ends]
+    sums[my_draw] = jnp.concatenate(packed, axis=0)
+
+    lax.fori_loop(0, TSHIFT // 64, table_rows, 0)
     pl.semaphore_wait(barrier, n_all - 1)
 
     def sum_copy(slot, dev):
@@ -126,18 +150,9 @@
 
     each(n_draw - 1, lambda r: sum_copy(my_draw, lax.rem(my_draw + 1 + r, n_draw)).start())
 
-    def table_rows(i, carry):
-        at = pl.multiple_of(i * 16, 16)
-        odd = (2 * (lax.broadcasted_iota(jnp.int32, (16, bins), 0) + at) + 1).astype(F32)
-        c, s = cos_sin_turns(odd * upper_row * turns)
-        ch, cl = halves(c)
-        sh, sl = halves(s)
-        ctab[pl.ds(at, 16), :] = jnp.concatenate([ch, ch, cl, cl], axis=1)
-        stab[pl.ds(at, 16), :] = jnp.concatenate([sh, sh, sl, sl], axis=1)
-        return carry
-
-    lax.fori_loop(0, TSHIFT // 32, table_rows, 0)
-
+    lax.fori_loop(TSHIFT // 64, TSHIFT // 32, table_rows, 0)
+    for load in loads[3:]:
+        load.wait()
     mine = pl.ds(pl.multiple_of(my_bin * half, half), half)
     amp = [jnp.exp(amp_ref[d:d + 1, mine]) for d in range(dets)]
     delay = [delay_ref[d:d + 1, mine] for d in range(dets)]
@@ -171,16 +186,14 @@
     for i in range(1, n_draw):
         total = total + sums[i]
 
-    start, end = total[:2 * dets], total[2 * dets:4 * dets]
-    both = end + jnp.where(lane_row < bins - 1, pltpu.roll(total, bins - 1, 1)[:2 * dets], 0.0)
     rc, rs = cos_sin_turns(upper_row * turns)
     rc, rs = rc * LOG2E, rs * LOG2E
     rows = []
     for d in range(dets):
-        re, im = both[2 * d:2 * d + 1], both[2 * d + 1:2 * d + 2]
+        re, im = total[2 * d:2 * d + 1], total[2 * d + 1:2 * d + 2]
         rows += [re * rc - im * rs, im * rc + re * rs]
-    rows += [total[4 * dets + d:4 * dets + d + 1] for d in range(dets)]
-    rows.append(jnp.zeros((LANES - len(rows), bins), F32))
+    rows.append(total[2 * dets:3 * dets])
+    rows.append(jnp.zeros((LANES - 3 * dets, bins), F32))
     coef[...] = jnp.concatenate(rows, axis=0).T
 
     zero = jnp.zeros((8, half), F32)
@@ -207,9 +220,11 @@
 
     self_power = jnp.sum(lax.fori_loop(0, bins // 16, mix_rows, zero), axis=0, keepdims=True)
     fixed = jnp.zeros((1, half), F32)
+    misc = total[3 * dets:3 * dets + 1]
     for d in range(dets):
-        self_power = self_power + (0.5 * twice[d]) * total[ROWS - 1:ROWS, d:d + 1]
-        fixed = fixed + amp[d] * (start[2 * d:2 * d + 1, 0:1] * cos0 + start[2 * d + 1:2 * d + 2, 0:1] * sin0)
+        self_power = self_power + (0.5 * twice[d]) * misc[:, d:d + 1]
+        at = dets + 2 * d
+        fixed = fixed + amp[d] * (misc[:, at:at + 1] * cos0 + misc[:, at + 1:at + 2] * sin0)
     base_ref[...] = fixed - 0.5 * self_power + prop_ref[:, mine] - math.log(TSHIFT)
 
     top = jnp.full((8, half), -jnp.inf, F32)
@@ -229,31 +244,36 @@
 
     largest = jnp.max(marginal, axis=1, keepdims=True)
     scaled = jnp.sum(jnp.exp(marginal - largest), axis=1, keepdims=True)
-    count = half // LANES
-    used = [marginal[:, i * LANES:(i + 1) * LANES] for i in range(count)]
-    used += [jnp.broadcast_to(largest, (1, LANES)), jnp.broadcast_to(scaled, (1, LANES))]
-    pad = packets.shape[1] - len(used)
-    packets[me] = jnp.concatenate(used + [jnp.zeros((pad, LANES), F32)], axis=0)
-
-    def packet_copy(slot, dev):
+    lane = lax.broadcasted_iota(jnp.int32, (1, LANES), 1)
+    stats[me] = jnp.where(lane < LANES // 2, largest, scaled)
+    margs[my_bin] = marginal
+
+    def stat_copy(slot, dev):
         return pltpu.make_async_remote_copy(
-            src_ref=packets.at[slot], dst_ref=packets.at[slot], send_sem=send2.at[dev], recv_sem=recv2.at[slot],
+            src_ref=stats.at[slot], dst_ref=stats.at[slot], send_sem=send2.at[dev], recv_sem=recv2.at[slot],
             device_id={"draw": dev // n_bin, "bin": lax.rem(dev, n_bin)}, device_id_type=pl.DeviceIdType.MESH)
 
-    each(n_all - 1, lambda r: packet_copy(me, lax.rem(me + 1 + r, n_all)).start())
-    each(n_all - 1, lambda r: packet_copy(lax.rem(me + 1 + r, n_all), me).wait_recv())
-
-    tops = packets[:, count, :]
-    masses = packets[:, count + 1, :]
-    whole_top = jnp.max(tops, axis=0, keepdims=True)
-    whole = jnp.sum(masses * jnp.exp(tops - whole_top), axis=0, keepdims=True)
-    total_log = whole_top + jnp.log(whole)
+    def marg_copy(slot, dev):
+        return pltpu.make_async_remote_copy(
+            src_ref=margs.at[slot], dst_ref=margs.at[slot], send_sem=send3.at[dev], recv_sem=recv3.at[slot],
+            device_id={"draw": my_draw, "bin": dev}, device_id_type=pl.DeviceIdType.MESH)
+
+    each(n_all - 1, lambda r: stat_copy(me, lax.rem(me + 1 + r, n_all)).start())
+    each(n_bin - 1, lambda r: marg_copy(my_bin, lax.rem(my_bin + 1 + r, n_bin)).start())
+    each(n_all - 1, lambda r: stat_copy(lax.rem(me + 1 + r, n_all), me).wait_recv())
+
+    tops = [stats[i] for i in range(n_all)]
+    whole_top = functools.reduce(jnp.maximum, tops)
+    whole = functools.reduce(jnp.add, [pltpu.roll(x, LANES // 2, 1) * jnp.exp(x - whole_top) for x in tops])
+    total_log = (whole_top + jnp.log(whole))[:, 0:1]
+    evid_ref[...] = total_log - math.log(half * n_all)
+    each(n_bin - 1, lambda r: marg_copy(lax.rem(my_bin + 1 + r, n_bin), my_bin).wait_recv())
     for q in range(n_bin):
-        out_ref[q * count:(q + 1) * count, :] = packets[my_draw * n_bin + q, 0:count, :] - total_log
-    evid_ref[...] = total_log[:, 0:1] - math.log(half * n_all)
+        out_ref[:, q * half:(q + 1) * half] = margs[q] - total_log
 
     each(n_draw - 1, lambda r: sum_copy(my_draw, lax.rem(my_draw + 1 + r, n_draw)).wait_send())
-    each(n_all - 1, lambda r: packet_copy(me, lax.rem(me + 1 + r, n_all)).wait_send())
+    each(n_all - 1, lambda r: stat_copy(me, lax.rem(me + 1 + r, n_all)).wait_send())
+    each(n_bin - 1, lambda r: marg_copy(my_bin, lax.rem(my_bin + 1 + r, n_bin)).wait_send())
 
 
 def body(n_draw, n_bin, fine_cross, fine_power, bin_widths, log_amps, delays, phases, chirps, proposal_log):
@@ -262,16 +282,24 @@
     draws = phases.shape[0]
     half = draws // n_bin
     n_all = n_draw * n_bin
-    packet_rows = -(-(half // LANES + 2) // 8) * 8
     vmem = pl.BlockSpec(memory_space=pltpu.VMEM)
     weights, evidence = pl.pallas_call(
         functools.partial(kernel, n_draw, n_bin),
-        out_shape=(jax.ShapeDtypeStruct((draws // LANES, LANES), F32), jax.ShapeDtypeStruct((1, 1), F32)),
-        in_specs=[vmem] * 8,
+        out_shape=(pltpu.VMEM((1, draws), F32), jax.ShapeDtypeStruct((1, 1), F32)),
+        in_specs=[pl.BlockSpec(memory_space=pltpu.HBM)] * 8,
         out_specs=(vmem, vmem),
         scratch_shapes=[
-            pltpu.VMEM((n_draw, ROWS, bins), F32),
-            pltpu.VMEM((n_all, packet_rows, LANES), F32),
+            pltpu.VMEM(fine_cross.shape, F32),
+            pltpu.VMEM(fine_power.shape, F32),
+            pltpu.VMEM((1, bins), jnp.int32),
+            pltpu.VMEM(log_amps.shape, F32),
+            pltpu.VMEM(delays.shape, F32),
+            pltpu.VMEM((1, draws), F32),
+            pltpu.VMEM((1, draws), F32),
+            pltpu.VMEM((1, draws), F32),
+            pltpu.VMEM((n_draw, 3 * dets + 1, bins), F32),
+            pltpu.VMEM((n_all, 1, LANES), F32),
+            pltpu.VMEM((n_bin, 1, half), F32),
             pltpu.VMEM((TSHIFT // 2, 4 * bins), BF16),
             pltpu.VMEM((TSHIFT // 2, 4 * bins), BF16),
             pltpu.VMEM((dets, bins, half), F32),
@@ -282,10 +310,13 @@
             pltpu.VMEM((bins, LANES), F32),
             pltpu.VMEM((bins, LANES), F32),
             pltpu.VMEM((1, half), F32),
+            pltpu.SemaphoreType.DMA((8,)),
             pltpu.SemaphoreType.DMA((n_draw,)),
             pltpu.SemaphoreType.DMA((n_draw,)),
             pltpu.SemaphoreType.DMA((n_all,)),
             pltpu.SemaphoreType.DMA((n_all,)),
+            pltpu.SemaphoreType.DMA((n_bin,)),
+            pltpu.SemaphoreType.DMA((n_bin,)),
         ],
         compiler_params=pltpu.CompilerParams(collective_id=0, has_side_effects=True),
         name="evidence",

time: 23 us -> 21.3 us (0.926)
  Pallas kernels: 19 us -> 18.2 us
  local copies, waits for them, and re-layouts: 1.26 us -> 0.6 us
    pallas_call x1, Pallas kernels: 19 us -> 18.2 us  [body(): pl.pallas_call(functools.partial(kernel, n_draw, n_bin), out_shape=(pltpu...]
    unnamed x3 -> x1, local copies, waits for them, and re-layouts: 1.26 us -> 0.6 us
where the time goes in v2:
time: 21.3 us; the launch traced here: 21.1 us
  Pallas kernels  18.2 us (85%)
  between operations  2.33 us (11%)
  local copies, waits for them, and re-layouts  0.6 us (3%)
    pallas_call x1, Pallas kernels, body(): pl.pallas_call(functools.partial(kernel, n_draw, n_bin), out_shape=(pltpu...  18.2 us
    unnamed x1, local copies, waits for them, and re-layouts  0.6 us

profile of v2, /device:TPU:0, one launch (start us, length us, event | category | flops | bytes accessed | tf_op | source)
XLA Modules:
  0.0 21.1 jit_solution(12955069366988595770)
XLA Ops:
  0.6 18.2 %evidence.1 = (f32[1,1024]{1,0:T(1,128)S(1)}, f32[1,1]{1,0:T(1,128)}) custom-call(f32[3,2,1024]{2,1,0:T(2,128)} %cross_in.1, f32[3,1024]{1,0:T(4,128)} %power_in.1, s32[1,128]{1,0:T(1,128)} %bitcast.10, f32[3,1024]{1,0:T(4,128)} %amp_in.1, f32[3,1024]{1,0:T(4,128)} %delay_in.1, f32[1,1024]{1,0:T(1,128)} %bitcast.7, f32[1,1024]{1,0:T(1,128)} %bitcast.8, ...), custom_call_target="tpu_custom_call" | custom-call | tf_op jit(solution)/shard_map/evidence/pallas_call | solution.py:286
  18.8 0.6 %copy.12 = f32[1024]{0:T(1024)} copy(f32[1024]{0:T(1024)S(1)} %bitcast.6) | data formatting | bytes 8192

commit v3 on v2

--- a/solution.py
+++ b/solution.py
@@ -61,7 +61,7 @@
 
 
 def kernel(n_draw, n_bin, cross_in, power_in, width_in, amp_in, delay_in, phase_in, chirp_in, prop_in,
-           out_ref, evid_ref, cross_ref, power_ref, width_ref, amp_ref, delay_ref, phase_ref, chirp_ref, prop_ref,
+           out_ref, cross_ref, power_ref, width_ref, amp_ref, delay_ref, phase_ref, chirp_ref, prop_ref,
            sums, stats, margs, ctab, stab, acos, asin, cdiff, zr, zi, xcol, coef, base_ref,
            load_sem, send1, recv1, send2, recv2, send3, recv3):
     loads = [pltpu.make_async_copy(src, dst, load_sem.at[i]) for i, (src, dst) in enumerate((
@@ -266,7 +266,7 @@
     whole_top = functools.reduce(jnp.maximum, tops)
     whole = functools.reduce(jnp.add, [pltpu.roll(x, LANES // 2, 1) * jnp.exp(x - whole_top) for x in tops])
     total_log = (whole_top + jnp.log(whole))[:, 0:1]
-    evid_ref[...] = total_log - math.log(half * n_all)
+    out_ref[:, n_bin * half:] = jnp.broadcast_to(total_log - math.log(half * n_all), (1, LANES))
     each(n_bin - 1, lambda r: marg_copy(lax.rem(my_bin + 1 + r, n_bin), my_bin).wait_recv())
     for q in range(n_bin):
         out_ref[:, q * half:(q + 1) * half] = margs[q] - total_log
@@ -283,11 +283,11 @@
     half = draws // n_bin
     n_all = n_draw * n_bin
     vmem = pl.BlockSpec(memory_space=pltpu.VMEM)
-    weights, evidence = pl.pallas_call(
+    both = pl.pallas_call(
         functools.partial(kernel, n_draw, n_bin),
-        out_shape=(pltpu.VMEM((1, draws), F32), jax.ShapeDtypeStruct((1, 1), F32)),
+        out_shape=pltpu.VMEM((1, draws + LANES), F32),
         in_specs=[pl.BlockSpec(memory_space=pltpu.HBM)] * 8,
-        out_specs=(vmem, vmem),
+        out_specs=vmem,
         scratch_shapes=[
             pltpu.VMEM(fine_cross.shape, F32),
             pltpu.VMEM(fine_power.shape, F32),
@@ -322,7 +322,7 @@
         name="evidence",
     )(fine_cross, fine_power, bin_widths.reshape(1, bins), log_amps, delays, phases.reshape(1, draws),
       chirps.reshape(1, draws), proposal_log.reshape(1, draws))
-    return weights.reshape(draws), evidence.reshape(1)
+    return both[0, :draws], both[0, draws:draws + 1]
 
 
 def solution(mesh):

time: 21.3 us -> 19.6 us (0.920)
  between operations: 2.33 us -> 0.64 us
  local copies, waits for them, and re-layouts: 0.6 us -> 1.11 us
  Pallas kernels: 18.2 us -> 17.7 us
    slice x0 -> x2, local copies, waits for them, and re-layouts: none -> 1.11 us  [body(): return (both[0, :draws], both[0, draws:draws + 1])]
    unnamed x1 -> x0, local copies, waits for them, and re-layouts: 0.6 us -> none
    pallas_call x1, Pallas kernels: 18.2 us -> 17.7 us  [body(): pl.pallas_call(functools.partial(kernel, n_draw, n_bin), out_shape=pltpu....]
where the time goes in v3:
time: 19.6 us; the launch traced here: 19.5 us
  Pallas kernels  17.7 us (90%)
  local copies, waits for them, and re-layouts  1.11 us (6%)
  between operations  0.64 us (3%)
    pallas_call x1, Pallas kernels, body(): pl.pallas_call(functools.partial(kernel, n_draw, n_bin), out_shape=pltpu....  17.7 us
    slice x2, local copies, waits for them, and re-layouts, body(): return (both[0, :draws], both[0, draws:draws + 1])  1.11 us

profile of v3, /device:TPU:0, one launch (start us, length us, event | category | flops | bytes accessed | tf_op | source)
XLA Modules:
  0.0 19.5 jit_solution(1048285863467611080)
XLA Ops:
  0.6 17.7 %evidence.1 = f32[1,1152]{1,0:T(1,128)S(1)} custom-call(f32[3,2,1024]{2,1,0:T(2,128)} %cross_in.1, f32[3,1024]{1,0:T(4,128)} %power_in.1, s32[1,128]{1,0:T(1,128)} %bitcast.10, f32[3,1024]{1,0:T(4,128)} %amp_in.1, f32[3,1024]{1,0:T(4,128)} %delay_in.1, f32[1,1024]{1,0:T(1,128)} %bitcast.6, f32[1,1024]{1,0:T(1,128)} %bitcast.7, f32[1,1024]{1,0:T(1,128)} %bitcast.8), custom_call_target="tpu_custom_call" | custom-call | tf_op jit(solution)/shard_map/evidence/pallas_call | solution.py:286
  18.4 0.5 %slice.7 = f32[1,1]{1,0:T(1,128)} slice(f32[1,1152]{1,0:T(1,128)S(1)} %evidence.1), slice={[0:1], [1024:1025]} | slice | bytes 8 | tf_op jit(solution)/shard_map/slice | solution.py:325
  18.9 0.6 %slice.6 = f32[1,1024]{1,0:T(1,128)} slice(f32[1,1152]{1,0:T(1,128)S(1)} %evidence.1), slice={[0:1], [0:1024]} | slice | bytes 8192 | tf_op jit(solution)/shard_map/slice | solution.py:325
